TPU v7x, 32 devices: a whole 2x2x4 slice. The times are simulated.
32 devices in a mesh: grp: 2 (over core), dom: 16 (over z, y, x).
Axes of the slice: x: 2, y: 2, z: 4, core: 2. Of those that a mesh axis runs over, the one named last changes fastest.
Arguments:
- node_latent: bfloat16 [32768, 128], P(('grp', 'dom')), may hold values from -6 to 6
- edge_latent: bfloat16 [196608, 128], P(('grp', 'dom')), may hold values from -6 to 6
- mig_send: int32 [32, 256], P(('grp', 'dom')), may hold values from 0 to 1024, as said below
- mig_recv: int32 [32768], P(('grp', 'dom')), may hold values from 0 to 1279, as said below
- halo_send: int32 [32, 128], P(('grp', 'dom')), may hold values from 0 to 1024, as said below
- cross_send: int32 [32, 32], P(('grp', 'dom')), may hold values from 0 to 1024, as said below
- senders: int32 [196608], P(('grp', 'dom')), may hold values from 0 to 1183, as said below
- receivers: int32 [196608], P(('grp', 'dom')), may hold values from 0 to 1023
- edge_live: int32 [196608], P(('grp', 'dom')), may hold values from 0 to 1, as said below
- edge_w1: bfloat16 [384, 128], replicated, may hold values from -0.3125 to 0.3125
- edge_b1: float32 [128], replicated, may hold values from -2 to 2
- edge_w2: bfloat16 [128, 128], replicated, may hold values from -0.5 to 0.5
- edge_b2: float32 [128], replicated, may hold values from -2 to 2
- edge_gain: float32 [128], replicated, may hold values from 0.25 to 1.75
- edge_bias: float32 [128], replicated, may hold values from -2 to 2
- node_w1: bfloat16 [256, 128], replicated, may hold values from -0.375 to 0.375
- node_b1: float32 [128], replicated, may hold values from -2 to 2
- node_w2: bfloat16 [128, 128], replicated, may hold values from -0.5 to 0.5
- node_b2: float32 [128], replicated, may hold values from -2 to 2
- node_gain: float32 [128], replicated, may hold values from 0.25 to 1.75
- node_bias: float32 [128], replicated, may hold values from -2 to 2
Outputs:
- node_out: bfloat16 [32768, 128], P(('grp', 'dom'))
- edge_out: bfloat16 [196608, 128], P(('grp', 'dom'))
Inputs may be any that keep to these rules, and one draw needn't show every extreme that they name: `mig_send`: per partition, slot k * 64 + c names an old local row moving to the partition at distance o_k, or 1024 for an empty slot; live slots of one distance come first, every old row is named at most once, and a partition sends to a partition exactly as many rows as it receives from it. Where the peer exists, 32 or more slots of a distance are live; slots toward missing partitions are empty; in every draw some partition of each region fills all its slots both ways. `mig_recv`: for each partition, 1024 distinct entries of its source table: old rows it did not send and live arrived slots, each exactly once. `halo_send`: slot k * 32 + c names a new local row sent to the partition at distance o_k, or 1024 if empty; live slots come first, rows are distinct within a partition; where the peer exists 32 // 2 or more are live, and some partition of each region fills all slots whose peer exists. `cross_send`: new local rows sent to the same partition of the other region, or 1024 if empty; live slots come first, 16 or more live, distinct from that partition's halo_send rows; some partition of each region fills all. `senders`: each entry names a new local row (below 1024) or a live halo or cross slot of the extended table. `edge_live`: within a partition, the live edge slots are a prefix of at least 3072 slots; some partition is fully live in every draw.
All inputs are finite; a program needn't handle non-finite values.
Results may differ from a plain program's by a relative error of at most 0.0075.
Values may be sent and summed in bfloat16 or wider, within the bound.
No kernel may reach another device: no remote copies, remote signals or barrier semaphores. Data moves between devices by JAX's collectives and lax.ppermute only.
A program may use at most 64 MiB of HBM per device.

v0:
```python
import jax
import jax.numpy as jnp
from jax import lax
from jax.sharding import PartitionSpec as P

R = 2
TILE = 128


EPSILON = 1e-05


def passed_along(value, axis, steps):
    count = lax.axis_size(axis)
    first, last = (max(0, -steps), min(count, count - steps))
    return lax.ppermute(value, axis, [(source, source + steps) for source in range(first, last)])


def swapped(value, axis, distance):
    return lax.ppermute(value, axis, [(i, i ^ 1 << distance) for i in range(lax.axis_size(axis))])


def offset_list():
    return [number - R if number < R else number - R + 1 for number in range(2 * R)]


def layer_norm(values, scale_vec, offset_vec):
    center = values - jnp.mean(values, axis=-1, keepdims=True)
    spread = jnp.mean(center * center, axis=-1, keepdims=True)
    return center * lax.rsqrt(spread + EPSILON) * scale_vec + offset_vec


def select_rows(source_rows, wanted):
    marks = (wanted[:, None] == jnp.arange(source_rows.shape[0], dtype=jnp.int32)[None, :]).astype(
        jnp.bfloat16
    )
    return jnp.dot(marks, source_rows, preferred_element_type=jnp.float32).astype(jnp.bfloat16)


def body(
    node_latent,
    edge_latent,
    mig_send,
    mig_recv,
    halo_send,
    cross_send,
    senders,
    receivers,
    edge_live,
    edge_w1,
    edge_b1,
    edge_w2,
    edge_b2,
    edge_gain,
    edge_bias,
    node_w1,
    node_b1,
    node_w2,
    node_b2,
    node_gain,
    node_bias,
):
    latent = node_latent.shape[1]
    node_count = node_latent.shape[0]
    distances = 2 * R
    move_slots = mig_send.shape[1] // distances
    halo_slots = halo_send.shape[1] // distances
    leaving = select_rows(node_latent, mig_send.reshape(-1)).reshape(distances, move_slots, latent)
    arrived = jnp.concatenate(
        [passed_along(leaving[place], "dom", shift) for place, shift in enumerate(offset_list())],
        axis=0,
    )
    source_rows = jnp.concatenate([node_latent, arrived], axis=0)
    fresh = select_rows(source_rows, mig_recv)
    halo_out = select_rows(fresh, halo_send.reshape(-1)).reshape(distances, halo_slots, latent)
    halo_in = jnp.concatenate(
        [passed_along(halo_out[place], "dom", shift) for place, shift in enumerate(offset_list())],
        axis=0,
    )
    cross_in = swapped(select_rows(fresh, cross_send.reshape(-1)), "grp", 0)
    extended = jnp.concatenate([fresh, halo_in, cross_in], axis=0)
    block_rows = 4 * TILE
    blocks = edge_latent.shape[0] // block_rows
    node_ids = jnp.arange(node_count, dtype=jnp.int32)

    def edge_block(inbound, pieces):
        edge_rows, sender_ids, receiver_ids, active = pieces
        sent_side = select_rows(extended, sender_ids)
        marks = (receiver_ids[:, None] == node_ids[None, :]).astype(jnp.bfloat16)
        recv_side = jnp.dot(marks, fresh, preferred_element_type=jnp.float32).astype(jnp.bfloat16)
        joined = jnp.concatenate([edge_rows, sent_side, recv_side], axis=1)
        hidden = jnp.maximum(
            jnp.dot(joined, edge_w1, preferred_element_type=jnp.float32) + edge_b1, 0.0
        ).astype(jnp.bfloat16)
        before = jnp.dot(hidden, edge_w2, preferred_element_type=jnp.float32) + edge_b2
        message = layer_norm(before, edge_gain, edge_bias).astype(jnp.bfloat16)
        kept = message * active.astype(jnp.bfloat16)[:, None]
        inbound = inbound + lax.dot_general(
            marks, kept, (((0,), (0,)), ((), ())), preferred_element_type=jnp.float32
        )
        updated = (edge_rows.astype(jnp.float32) + kept.astype(jnp.float32)).astype(jnp.bfloat16)
        return (inbound, updated)

    inbound, updated = lax.scan(
        edge_block,
        jnp.zeros((node_count, latent), jnp.float32),
        (
            edge_latent.reshape(blocks, block_rows, latent),
            senders.reshape(blocks, block_rows),
            receivers.reshape(blocks, block_rows),
            edge_live.reshape(blocks, block_rows),
        ),
    )
    node_in = jnp.concatenate([fresh, inbound.astype(jnp.bfloat16)], axis=1)
    node_hidden = jnp.maximum(
        jnp.dot(node_in, node_w1, preferred_element_type=jnp.float32) + node_b1, 0.0
    ).astype(jnp.bfloat16)
    node_before = jnp.dot(node_hidden, node_w2, preferred_element_type=jnp.float32) + node_b2
    node_out = (fresh.astype(jnp.float32) + layer_norm(node_before, node_gain, node_bias)).astype(
        jnp.bfloat16
    )
    return (node_out, updated.reshape(-1, latent))


def solution(mesh):
    placed = (
        P(("grp", "dom"), None),
        P(("grp", "dom"), None),
        P(("grp", "dom"), None),
        P(("grp", "dom")),
        P(("grp", "dom"), None),
        P(("grp", "dom"), None),
        P(("grp", "dom")),
        P(("grp", "dom")),
        P(("grp", "dom")),
        P(),
        P(),
        P(),
        P(),
        P(),
        P(),
        P(),
        P(),
        P(),
        P(),
        P(),
        P(),
    )
    return jax.shard_map(
        body,
        mesh=mesh,
        in_specs=placed,
        out_specs=(P(("grp", "dom"), None), P(("grp", "dom"), None)),
        check_vma=False,
    )
```

profile of v0, /device:TPU:0, one launch (start us, length us, event | category | flops | bytes accessed | tf_op | source)
XLA Modules:
  0.0 97.1 jit_solution(11773821220590536432)
XLA Ops:
  0.7 1.4 %convolution_convert_fusion = bf16[256,128]{1,0:T(8,128)(2,1)S(1)} fusion(bf16[1024,128]{1,0:T(8,128)(2,1)} %param.23, s32[256]{0:T(256)} %bitcast.45), kind=kOutput, calls=%fused_computation.45 | convolution fusion | flops 67403776 | bytes 328704 | tf_op jit(solution)/shard_map/dot_general | solution.py:37
  2.0 4.9 %collective-permute-start.3 = (bf16[64,128]{1,0:T(8,128)(2,1)S(1)}, bf16[64,128]{1,0:T(8,128)(2,1)S(1)}, u32[]{:S(2)}, u32[]{:S(2)}) collective-permute-start(bf16[64,128]{1,0:T(8,128)(2,1)S(1)} %get-tuple-element.186), channel_id=1, source_target_pairs={{0,2},{1,3},{2,4},{3,5},{4,6},{5,7},{6,8},{7,9},{8,10},{9,11},{10,... | collective-permute-start | bytes 49160 | tf_op jit(solution)/shard_map/ppermute | solution.py:16
  6.9 3.4 %collective-permute-start.2 = (bf16[64,128]{1,0:T(8,128)(2,1)S(1)}, bf16[64,128]{1,0:T(8,128)(2,1)S(1)}, u32[]{:S(2)}, u32[]{:S(2)}) collective-permute-start(bf16[64,128]{1,0:T(8,128)(2,1)S(1)} %get-tuple-element.187), channel_id=1, source_target_pairs={{0,1},{1,2},{2,3},{3,4},{4,5},{5,6},{6,7},{7,8},{8,9},{9,10},{10,1... | collective-permute-start | bytes 49160 | tf_op jit(solution)/shard_map/ppermute | solution.py:16
  10.3 1.3 %collective-permute-start.1 = (bf16[64,128]{1,0:T(8,128)(2,1)S(1)}, bf16[64,128]{1,0:T(8,128)(2,1)S(1)}, u32[]{:S(2)}, u32[]{:S(2)}) collective-permute-start(bf16[64,128]{1,0:T(8,128)(2,1)S(1)} %get-tuple-element.188), channel_id=1, source_target_pairs={{1,0},{2,1},{3,2},{4,3},{5,4},{6,5},{7,6},{8,7},{9,8},{10,9},{11,1... | collective-permute-start | bytes 49160 | tf_op jit(solution)/shard_map/ppermute | solution.py:16
  11.6 1.3 %collective-permute-start = (bf16[64,128]{1,0:T(8,128)(2,1)S(1)}, bf16[64,128]{1,0:T(8,128)(2,1)S(1)}, u32[]{:S(2)}, u32[]{:S(2)}) collective-permute-start(bf16[64,128]{1,0:T(8,128)(2,1)S(1)} %get-tuple-element.189), channel_id=1, source_target_pairs={{2,0},{3,1},{4,2},{5,3},{6,4},{7,5},{8,6},{9,7},{10,8},{11,9},{12,... | collective-permute-start | bytes 49160 | tf_op jit(solution)/shard_map/ppermute | solution.py:16
  12.9 1.0 constant_dynamic-update-slice_fusion.5
  16.2 2.7 %collective-permute-done = bf16[64,128]{1,0:T(8,128)(2,1)S(1)} collective-permute-done((bf16[64,128]{1,0:T(8,128)(2,1)S(1)}, bf16[64,128]{1,0:T(8,128)(2,1)S(1)}, u32[]{:S(2)}, u32[]{:S(2)}) %collective-permute-start) | collective-permute-done | bytes 16416 | tf_op jit(solution)/shard_map/ppermute | solution.py:16
  19.0 1.0 %constant_dynamic-update-slice_fusion.11 = (bf16[1184,128]{1,0:T(8,128)(2,1)S(1)}, bf16[1024,128]{1,0:T(8,128)(2,1)S(1)}) fusion(bf16[1280,128]{1,0:T(8,128)(2,1)S(1)} %constant_dynamic-update-slice_fusion.1, s32[1024]{0:T(1024)S(1)} %copy-done.8), kind=kOutput, calls=%fused_computation.71 | convolution fusion | flops 336986112 | bytes 856064 | tf_op jit(solution)/shard_map/dot_general | solution.py:37
  20.3 1.3 %collective-permute-start.4 = (bf16[32,128]{1,0:T(8,128)(2,1)S(1)}, bf16[32,128]{1,0:T(8,128)(2,1)S(1)}, u32[]{:S(2)}, u32[]{:S(2)}) collective-permute-start(bf16[32,128]{1,0:T(8,128)(2,1)S(1)} %get-tuple-element.193), channel_id=1, source_target_pairs={{2,0},{3,1},{4,2},{5,3},{6,4},{7,5},{8,6},{9,7},{10,8},{11,9},{12,... | collective-permute-start | bytes 24584 | tf_op jit(solution)/shard_map/ppermute | solution.py:16
  21.9 5.4 %collective-permute-start.7 = (bf16[32,128]{1,0:T(8,128)(2,1)S(1)}, bf16[32,128]{1,0:T(8,128)(2,1)S(1)}, u32[]{:S(2)}, u32[]{:S(2)}) collective-permute-start(bf16[32,128]{1,0:T(8,128)(2,1)S(1)} %get-tuple-element.190), channel_id=1, source_target_pairs={{0,2},{1,3},{2,4},{3,5},{4,6},{5,7},{6,8},{7,9},{8,10},{9,11},{10,... | collective-permute-start | bytes 24584 | tf_op jit(solution)/shard_map/ppermute | solution.py:16
  27.4 2.5 %collective-permute-start.6 = (bf16[32,128]{1,0:T(8,128)(2,1)S(1)}, bf16[32,128]{1,0:T(8,128)(2,1)S(1)}, u32[]{:S(2)}, u32[]{:S(2)}) collective-permute-start(bf16[32,128]{1,0:T(8,128)(2,1)S(1)} %get-tuple-element.191), channel_id=1, source_target_pairs={{0,1},{1,2},{2,3},{3,4},{4,5},{5,6},{6,7},{7,8},{8,9},{9,10},{10,1... | collective-permute-start | bytes 24584 | tf_op jit(solution)/shard_map/ppermute | solution.py:16
  29.9 1.3 %collective-permute-start.5 = (bf16[32,128]{1,0:T(8,128)(2,1)S(1)}, bf16[32,128]{1,0:T(8,128)(2,1)S(1)}, u32[]{:S(2)}, u32[]{:S(2)}) collective-permute-start(bf16[32,128]{1,0:T(8,128)(2,1)S(1)} %get-tuple-element.192), channel_id=1, source_target_pairs={{1,0},{2,1},{3,2},{4,3},{5,4},{6,5},{7,6},{8,7},{9,8},{10,9},{11,1... | collective-permute-start | bytes 24584 | tf_op jit(solution)/shard_map/ppermute | solution.py:16
  31.2 6.0 %collective-permute-done.5 = bf16[32,128]{1,0:T(8,128)(2,1)S(1)} collective-permute-done((bf16[32,128]{1,0:T(8,128)(2,1)S(1)}, bf16[32,128]{1,0:T(8,128)(2,1)S(1)}, u32[]{:S(2)}, u32[]{:S(2)}) %collective-permute-start.5) | collective-permute-done | bytes 8224 | tf_op jit(solution)/shard_map/ppermute | solution.py:16
  37.4 57.6 %while.13 = (s32[]{:T(128)}, f32[1024,128]{1,0:T(8,128)S(1)}, bf16[12,512,128]{2,1,0:T(8,128)(2,1)}, s32[12,512]{1,0:T(8,128)S(1)}, bf16[12,512,128]{2,1,0:T(8,1...) while((s32[]{:T(128)}, f32[1024,128]{1,0:T(8,128)S(1)}, ...), condition=%wide.region_3.4_spmd.clone, body=%wide.region_0.3_spmd.clone.sunk | while | flops 496059392 | bytes 4804799 | solution.py:104
  38.9 0.9 constant_dynamic-slice_fusion.6
  43.7 0.9 constant_dynamic-slice_fusion.6
  48.5 0.9 constant_dynamic-slice_fusion.6
  53.3 0.9 constant_dynamic-slice_fusion.6
  58.1 0.9 constant_dynamic-slice_fusion.6
  62.9 0.9 constant_dynamic-slice_fusion.6
  67.7 0.9 constant_dynamic-slice_fusion.6
  72.5 0.9 constant_dynamic-slice_fusion.6
  77.3 0.9 constant_dynamic-slice_fusion.6
  96.1 1.0 %add_convert_fusion.2 = bf16[1024,128]{1,0:T(8,128)(2,1)} fusion(bf16[1024,128]{1,0:T(8,128)(2,1)S(1)} %get-tuple-element.348, f32[1024,128]{1,0:T(8,128)S(1)} %get-tuple-element.197, f32[128]{0:T(128)S(1)} %copy-done.3, f32[128]{0:T(128)S(1)} %copy-done.4, f32[1024]{0:T(1024)S(1)} %add_rsqrt_fusion.1, f32[1024]{0:T(1024)S(1)} %broadcast_multiply_fusion.1), kind=kLoop, calls=%fused_computation.52 | loop fusion | flops 917504 | bytes 1057792 | tf_op jit(solution)/shard_map/convert_element_type | solution.py:119
  (220 shorter events, 52.5 us)
Async XLA Ops:
  0.6 94.4 %copy-start = (bf16[256,128]{1,0:T(8,128)(2,1)S(1)}, bf16[256,128]{1,0:T(8,128)(2,1)}, u32[]{:S(2)}) copy-start(bf16[256,128]{1,0:T(8,128)(2,1)} %param.38) | copy-start | bytes 196612
  0.6 18.3 %copy-start.8 = (s32[1024]{0:T(1024)S(1)}, s32[1024]{0:T(1024)}, u32[]{:S(2)}) copy-start(s32[1024]{0:T(1024)} %param.26) | copy-start | bytes 12292
  2.0 16.9 %collective-permute-start.3 = (bf16[64,128]{1,0:T(8,128)(2,1)S(1)}, bf16[64,128]{1,0:T(8,128)(2,1)S(1)}, u32[]{:S(2)}, u32[]{:S(2)}) collective-permute-start(bf16[64,128]{1,0:T(8,128)(2,1)S(1)} %get-tuple-element.186), channel_id=1, source_target_pairs={{0,2},{1,3},{2,4},{3,5},{4,6},{5,7},{6,8},{7,9},{8,10},{9,11},{10,... | collective-permute-start | bytes 49160 | tf_op jit(solution)/shard_map/ppermute | solution.py:16
  6.9 11.9 %collective-permute-start.2 = (bf16[64,128]{1,0:T(8,128)(2,1)S(1)}, bf16[64,128]{1,0:T(8,128)(2,1)S(1)}, u32[]{:S(2)}, u32[]{:S(2)}) collective-permute-start(bf16[64,128]{1,0:T(8,128)(2,1)S(1)} %get-tuple-element.187), channel_id=1, source_target_pairs={{0,1},{1,2},{2,3},{3,4},{4,5},{5,6},{6,7},{7,8},{8,9},{9,10},{10,1... | collective-permute-start | bytes 49160 | tf_op jit(solution)/shard_map/ppermute | solution.py:16
  10.3 8.5 %collective-permute-start.1 = (bf16[64,128]{1,0:T(8,128)(2,1)S(1)}, bf16[64,128]{1,0:T(8,128)(2,1)S(1)}, u32[]{:S(2)}, u32[]{:S(2)}) collective-permute-start(bf16[64,128]{1,0:T(8,128)(2,1)S(1)} %get-tuple-element.188), channel_id=1, source_target_pairs={{1,0},{2,1},{3,2},{4,3},{5,4},{6,5},{7,6},{8,7},{9,8},{10,9},{11,1... | collective-permute-start | bytes 49160 | tf_op jit(solution)/shard_map/ppermute | solution.py:16
  11.6 7.2 %collective-permute-start = (bf16[64,128]{1,0:T(8,128)(2,1)S(1)}, bf16[64,128]{1,0:T(8,128)(2,1)S(1)}, u32[]{:S(2)}, u32[]{:S(2)}) collective-permute-start(bf16[64,128]{1,0:T(8,128)(2,1)S(1)} %get-tuple-element.189), channel_id=1, source_target_pairs={{2,0},{3,1},{4,2},{5,3},{6,4},{7,5},{8,6},{9,7},{10,8},{11,9},{12,... | collective-permute-start | bytes 49160 | tf_op jit(solution)/shard_map/ppermute | solution.py:16
  14.7 5.4 %copy-start.9 = (s32[1,128]{1,0:T(1,128)S(1)}, s32[1,128]{1,0:T(1,128)}, u32[]{:S(2)}) copy-start(s32[1,128]{1,0:T(1,128)} %param.27) | copy-start | bytes 1540
  18.9 2.7 %copy-start.10 = (s32[1,32]{1,0:T(1,128)S(1)}, s32[1,32]{1,0:T(1,128)}, u32[]{:S(2)}) copy-start(s32[1,32]{1,0:T(1,128)} %param.28) | copy-start | bytes 388
  18.9 18.4 %copy-start.1 = (f32[128]{0:T(128)S(1)}, f32[128]{0:T(128)}, u32[]{:S(2)}) copy-start(f32[128]{0:T(128)} %param.36) | copy-start | bytes 1540
  18.9 18.4 %copy-start.2 = (f32[128]{0:T(128)S(1)}, f32[128]{0:T(128)}, u32[]{:S(2)}) copy-start(f32[128]{0:T(128)} %param.37) | copy-start | bytes 1540
  18.9 18.4 %copy-start.5 = (bf16[384,128]{1,0:T(8,128)(2,1)S(1)}, bf16[384,128]{1,0:T(8,128)(2,1)}, u32[]{:S(2)}) copy-start(bf16[384,128]{1,0:T(8,128)(2,1)} %param.32) | copy-start | bytes 294916
  19.0 18.4 %copy-start.6 = (bf16[128,128]{1,0:T(8,128)(2,1)S(1)}, bf16[128,128]{1,0:T(8,128)(2,1)}, u32[]{:S(2)}) copy-start(bf16[128,128]{1,0:T(8,128)(2,1)} %param.34) | copy-start | bytes 98308
  19.0 18.4 %copy-start.11 = (f32[128]{0:T(128)S(1)}, f32[128]{0:T(128)}, u32[]{:S(2)}) copy-start(f32[128]{0:T(128)} %param.33) | copy-start | bytes 1540
  19.0 18.4 %copy-start.12 = (f32[128]{0:T(128)S(1)}, f32[128]{0:T(128)}, u32[]{:S(2)}) copy-start(f32[128]{0:T(128)} %param.35) | copy-start | bytes 1540
  20.3 10.9 %collective-permute-start.4 = (bf16[32,128]{1,0:T(8,128)(2,1)S(1)}, bf16[32,128]{1,0:T(8,128)(2,1)S(1)}, u32[]{:S(2)}, u32[]{:S(2)}) collective-permute-start(bf16[32,128]{1,0:T(8,128)(2,1)S(1)} %get-tuple-element.193), channel_id=1, source_target_pairs={{2,0},{3,1},{4,2},{5,3},{6,4},{7,5},{8,6},{9,7},{10,8},{11,9},{12,... | collective-permute-start | bytes 24584 | tf_op jit(solution)/shard_map/ppermute | solution.py:16
  21.9 15.4 %collective-permute-start.8 = (bf16[32,128]{1,0:T(8,128)(2,1)S(1)}, bf16[32,128]{1,0:T(8,128)(2,1)S(1)}, u32[]{:S(2)}, u32[]{:S(2)}) collective-permute-start(bf16[32,128]{1,0:T(8,128)(2,1)S(1)} %convolution_convert_fusion.2), channel_id=1, source_target_pairs={{0,16},{16,0},{1,17},{17,1},{2,18},{18,2},{3,19},{19,3},{4,20},{20... | collective-permute-start | bytes 24584 | tf_op jit(solution)/shard_map/ppermute | solution.py:20
  21.9 15.3 %collective-permute-start.7 = (bf16[32,128]{1,0:T(8,128)(2,1)S(1)}, bf16[32,128]{1,0:T(8,128)(2,1)S(1)}, u32[]{:S(2)}, u32[]{:S(2)}) collective-permute-start(bf16[32,128]{1,0:T(8,128)(2,1)S(1)} %get-tuple-element.190), channel_id=1, source_target_pairs={{0,2},{1,3},{2,4},{3,5},{4,6},{5,7},{6,8},{7,9},{8,10},{9,11},{10,... | collective-permute-start | bytes 24584 | tf_op jit(solution)/shard_map/ppermute | solution.py:16
  27.4 9.8 %collective-permute-start.6 = (bf16[32,128]{1,0:T(8,128)(2,1)S(1)}, bf16[32,128]{1,0:T(8,128)(2,1)S(1)}, u32[]{:S(2)}, u32[]{:S(2)}) collective-permute-start(bf16[32,128]{1,0:T(8,128)(2,1)S(1)} %get-tuple-element.191), channel_id=1, source_target_pairs={{0,1},{1,2},{2,3},{3,4},{4,5},{5,6},{6,7},{7,8},{8,9},{9,10},{10,1... | collective-permute-start | bytes 24584 | tf_op jit(solution)/shard_map/ppermute | solution.py:16
  29.9 7.3 %collective-permute-start.5 = (bf16[32,128]{1,0:T(8,128)(2,1)S(1)}, bf16[32,128]{1,0:T(8,128)(2,1)S(1)}, u32[]{:S(2)}, u32[]{:S(2)}) collective-permute-start(bf16[32,128]{1,0:T(8,128)(2,1)S(1)} %get-tuple-element.192), channel_id=1, source_target_pairs={{1,0},{2,1},{3,2},{4,3},{5,4},{6,5},{7,6},{8,7},{9,8},{10,9},{11,1... | collective-permute-start | bytes 24584 | tf_op jit(solution)/shard_map/ppermute | solution.py:16
  37.3 57.7 %copy-start.7 = (bf16[128,128]{1,0:T(8,128)(2,1)S(1)}, bf16[128,128]{1,0:T(8,128)(2,1)}, u32[]{:S(2)}) copy-start(bf16[128,128]{1,0:T(8,128)(2,1)} %param.40) | copy-start | bytes 98308
  37.4 57.7 %copy-start.13 = (f32[128]{0:T(128)S(1)}, f32[128]{0:T(128)}, u32[]{:S(2)}) copy-start(f32[128]{0:T(128)} %param.41) | copy-start | bytes 1540
  37.4 57.7 %copy-start.14 = (f32[128]{0:T(128)S(1)}, f32[128]{0:T(128)}, u32[]{:S(2)}) copy-start(f32[128]{0:T(128)} %param.39) | copy-start | bytes 1540
  95.0 1.1 %copy-start.3 = (f32[128]{0:T(128)S(1)}, f32[128]{0:T(128)}, u32[]{:S(2)}) copy-start(f32[128]{0:T(128)} %param.43) | copy-start | bytes 1540
  95.0 1.1 %copy-start.4 = (f32[128]{0:T(128)S(1)}, f32[128]{0:T(128)}, u32[]{:S(2)}) copy-start(f32[128]{0:T(128)} %param.42) | copy-start | bytes 1540
where the time goes:
time: 97.9 us; the launch traced here: 97.1 us
  matrix products  35.6 us (36%)
  local copies, waits for them, and re-layouts  25.4 us (26%)
  starting transfers between devices  21.5 us (22%)
  waiting for transfers between devices  8.68 us (9%)
  other arithmetic  4.16 us (4%)
  between operations  1.04 us (1%)
    ppermute x8, starting transfers between devices, passed_along(): lax.ppermute(value, axis, [(source, source + steps) for source in range(f...  21.4 us
    dynamic_slice x36, local copies, waits for them, and re-layouts, body(): lax.scan(edge_block, jnp.zeros((node_count, latent), jnp.float32), (edge_...  12.5 us
    dot_general x16, matrix products, select_rows(): jnp.dot(marks, source_rows, preferred_element_type=jnp.float32)  11.8 us
    dot_general x12, matrix products, edge_block(): lax.dot_general(marks, kept, (((0,), (0,)), ((), ())), preferred_element_...  9.68 us
    dynamic_update_slice x24, local copies, waits for them, and re-layouts, body(): lax.scan(edge_block, jnp.zeros((node_count, latent), jnp.float32), (edge_...  9.45 us
    ppermute x8, waiting for transfers between devices, passed_along(): lax.ppermute(value, axis, [(source, source + steps) for source in range(f...  8.68 us
    dot_general x12, matrix products, edge_block(): jnp.dot(marks, fresh, preferred_element_type=jnp.float32)  7.68 us
    dot_general x12, matrix products, edge_block(): jnp.dot(hidden, edge_w2, preferred_element_type=jnp.float32) + edge_b2  5.79 us
  transfers between devices with their start and end apart: 9, of which 2 were waited for; matrix products, arithmetic and copies ran while one was open for 4% of the time, Pallas kernels for 0%

commit v1 on v0

v1 whole, which is shorter than its diff:
```python
import functools

import jax
import jax.numpy as jnp
from jax import lax
from jax.experimental import pallas as pl
from jax.experimental.pallas import tpu as pltpu
from jax.sharding import PartitionSpec as P

R = 2
LANES = 128
EDGE_BLOCK = 1024
ANY = pl.BlockSpec(memory_space=pl.ANY)
EPSILON = 1e-05
BF16 = jnp.bfloat16
F32 = jnp.float32


def dot(a, b):
    return jnp.dot(a, b, preferred_element_type=F32)


def swapped(value, axis, partner_of):
    count = lax.axis_size(axis)
    pairs = []
    for i in range(count):
        j = partner_of(i)
        pairs.append((i, j if 0 <= j < count else i))
    return lax.ppermute(value, axis, pairs)


def lane_ids(tile, shift):
    ids = lax.broadcasted_iota(jnp.int32, (LANES, LANES), 1) + (tile * LANES - shift)
    return ids.astype(F32).astype(BF16)


def spread(columns, b):
    return jnp.broadcast_to(columns[:, b : b + 1], (columns.shape[0], LANES))


def marks_from(values, count, shift):
    one, zero = jnp.ones((), BF16), jnp.zeros((), BF16)
    values = values.astype(BF16)
    rows = values.shape[0]
    return jnp.concatenate(
        [jnp.where(values == lane_ids(t, shift)[:rows], one, zero) for t in range(count)], axis=1
    )


def split_index(rows, half):
    high = (rows >= half).astype(F32)
    low = rows.astype(F32) - high * half - half // 2
    return low.T, high.T


def lookup(low, high, b, table2):
    half = table2.shape[0]
    both = dot(marks_from(spread(low, b), half // LANES, half // 2), table2)
    return jnp.where(spread(high, b) > 0.5, both[:, LANES:], both[:, :LANES])


def side_by_side(table):
    half = table.shape[0] // 2
    return jnp.concatenate([table[:half], table[half:]], axis=1)


def twice(w):
    zero = jnp.zeros_like(w)
    return jnp.concatenate(
        [jnp.concatenate([w, zero], axis=1), jnp.concatenate([zero, w], axis=1)], axis=0
    )


def eight(row):
    return jnp.broadcast_to(row, (8, row.shape[1]))


def leave_kernel(node_hbm, send_hbm, near_ref, far_ref, node_ref, send_ref, sems):
    copies = [
        pltpu.make_async_copy(send_hbm, send_ref, sems.at[0]),
        pltpu.make_async_copy(node_hbm, node_ref, sems.at[1]),
    ]
    for copy in copies:
        copy.start()
    for copy in copies:
        copy.wait()
    table = side_by_side(node_ref[...])
    pieces = []
    for b in range(send_ref.shape[1] // LANES):
        low, high = split_index(eight(send_ref[:, b * LANES : (b + 1) * LANES]), table.shape[0])
        pieces.append(lookup(low, high, 0, table))
    rows = jnp.concatenate(pieces, axis=0).astype(BF16)
    quarter = rows.shape[0] // 4
    near_ref[...] = rows[quarter : 3 * quarter]
    far_ref[...] = jnp.concatenate([rows[:quarter], rows[3 * quarter :]], axis=0)


def own_kernel(
    edge_ref, w1_ref, b1_ref, send_ref, recv_ref, live_ref, mig_ref, halo_ref, cross_ref, _,
    own_ref, w1_copy, send_copy, recv_copy, live_copy, mig_copy, halo_copy, cross_copy,
):
    w1_copy[...] = w1_ref[...]
    send_copy[...] = send_ref[...]
    recv_copy[...] = recv_ref[...]
    live_copy[...] = live_ref[...]
    mig_copy[...] = mig_ref[...]
    halo_copy[...] = halo_ref[...]
    cross_copy[...] = cross_ref[...]
    wa = twice(w1_ref[:LANES, :])
    b1 = b1_ref[...]
    half = EDGE_BLOCK // 2

    def step(i, carry):
        at = pl.multiple_of(i * EDGE_BLOCK, EDGE_BLOCK)
        top, bottom = edge_ref[pl.ds(at, half), :], edge_ref[pl.ds(at + half, half), :]
        pair = dot(jnp.concatenate([top, bottom], axis=1), wa)
        own_ref[pl.ds(at, half), :] = pair[:, :LANES] + b1
        own_ref[pl.ds(at + half, half), :] = pair[:, LANES:] + b1
        return carry

    lax.fori_loop(0, edge_ref.shape[0] // EDGE_BLOCK, step, 0)


def target_kernel(recv_ref, node_ref, _, marks_ref, table_ref):
    table_ref[...] = side_by_side(node_ref[...])
    half = marks_ref.shape[0]
    one, zero = jnp.ones((), BF16), jnp.zeros((), BF16)
    ids = (lax.broadcasted_iota(jnp.int32, (half, LANES), 0) - half // 2).astype(F32).astype(BF16)
    recv = recv_ref[...]
    low = jnp.where(recv >= half, recv - half, recv) - half // 2
    low = low.astype(F32)
    for b in range(recv.shape[0]):
        row = jnp.broadcast_to(low[b : b + 1, :], (16, LANES)).astype(BF16)
        row = jnp.concatenate([row] * (half // 16), axis=0)
        marks_ref[:, b * LANES : (b + 1) * LANES] = jnp.where(ids == row, one, zero)


def fresh_kernel(
    table_ref, arrived_ref, recv_ref, halo_ref, cross_ref, fresh_ref, near_ref, far_ref, cross_out
):
    table = table_ref[...]
    n = 2 * table.shape[0]
    recv = recv_ref[...]
    low, high = split_index(recv, table.shape[0])
    moved = (recv - n).astype(F32).T
    arrived = arrived_ref[...]
    pieces = []
    for b in range(n // LANES):
        marks = marks_from(spread(moved, b), arrived.shape[0] // LANES, 0)
        pieces.append((lookup(low, high, b, table) + dot(marks, arrived)).astype(BF16))
    fresh = jnp.concatenate(pieces, axis=0)
    fresh_ref[...] = fresh
    table = side_by_side(fresh)
    low, high = split_index(eight(halo_ref[...]), table.shape[0])
    halo = lookup(low, high, 0, table).astype(BF16)
    quarter = halo.shape[0] // 4
    near_ref[...] = halo[quarter : 3 * quarter]
    far_ref[...] = jnp.concatenate([halo[:quarter], halo[3 * quarter :]], axis=0)
    low, high = split_index(eight(cross_ref[...]), table.shape[0])
    cross_out[...] = lookup(low, high, 0, table).astype(BF16)


def pre_kernel(before_ref, fresh_ref, index_ref, w_ref, _, out_ref, *, part):
    table = side_by_side(dot(fresh_ref[...], w_ref[part * LANES : (part + 1) * LANES, :]).astype(BF16))

    def step(i, carry):
        low, high = split_index(
            index_ref[pl.ds(pl.multiple_of(i * 8, 8), 8), :], table.shape[0]
        )
        for b in range(EDGE_BLOCK // LANES):
            at = pl.ds(pl.multiple_of(i * EDGE_BLOCK + b * LANES, LANES), LANES)
            out_ref[at, :] = before_ref[at, :] + lookup(low, high, b, table)
        return carry

    lax.fori_loop(0, out_ref.shape[0] // EDGE_BLOCK, step, 0)


def edge_kernel(
    pre_ref, edge_ref, fresh_ref, halo_ref, cross_ref, send_ref, recv_ref, live_ref, target_ref,
    w1_ref, w2_ref, b2_ref, gain_ref, bias_ref,
    nw1_ref, nb1_ref, nw2_ref, nb2_ref, ngain_ref, nbias_ref,
    node_out_ref, edge_out_ref,
    new_ref, acc_ref, sems,
):
    n = fresh_ref.shape[0]
    block = EDGE_BLOCK
    half = block // 2
    blocks = block // LANES
    nodes_half = n // 2

    r = lax.broadcasted_iota(jnp.int32, (2 * LANES, 2 * LANES), 0) // LANES
    c = lax.broadcasted_iota(jnp.int32, (2 * LANES, 2 * LANES), 1) // LANES
    averages = jnp.where(r == c, 1.0 / LANES, 0.0).astype(BF16)
    b2 = b2_ref[...]
    b2 = b2 - jnp.mean(b2, axis=-1, keepdims=True)
    b2 = jnp.concatenate([b2, b2], axis=1)
    remote_rows = jnp.concatenate([halo_ref[...], cross_ref[...]], axis=0)
    tx = dot(remote_rows, w1_ref[LANES : 2 * LANES, :]).astype(BF16)
    tx = jnp.concatenate([tx, jnp.zeros((2 * LANES - tx.shape[0], LANES), BF16)], axis=0)
    w2 = w2_ref[...].astype(F32)
    w2 = twice((w2 - jnp.mean(w2, axis=-1, keepdims=True)).astype(BF16))
    gain, bias = gain_ref[...], bias_ref[...]
    acc_ref[...] = jnp.zeros_like(acc_ref)

    def copy_out(i):
        at = pl.ds(pl.multiple_of(i * block, block), block)
        return pltpu.make_async_copy(new_ref.at[at, :], edge_out_ref.at[at, :], sems.at[i])

    def step(i, carry):
        rows8 = pl.ds(pl.multiple_of(i * 8, 8), 8)
        remote = (send_ref[rows8, :] - n).astype(F32).T
        high = (recv_ref[rows8, :] >= nodes_half).astype(F32).T
        live = live_ref[rows8, :].astype(F32).T
        hidden = []
        for b in range(blocks):
            at = pl.ds(pl.multiple_of(i * block + b * LANES, LANES), LANES)
            pre = pre_ref[at, :] + dot(marks_from(spread(remote, b), 2, 0), tx)
            hidden.append(jnp.maximum(pre, 0.0).astype(BF16))
        packed = []
        for b in range(blocks // 2):
            both = jnp.concatenate([hidden[b], hidden[b + blocks // 2]], axis=1)
            centre = dot(both, w2) + b2
            spreads = dot((centre * centre).astype(BF16), averages)
            normed = centre * lax.rsqrt(spreads + EPSILON)
            for k in range(2):
                bb = b + k * (blocks // 2)
                at = pl.ds(pl.multiple_of(i * block + bb * LANES, LANES), LANES)
                message = normed[:, k * LANES : (k + 1) * LANES] * gain + bias
                kept = message.astype(BF16).astype(F32) * spread(live, bb)
                new_ref[at, :] = (edge_ref[at, :].astype(F32) + kept).astype(BF16)
                upper = kept * spread(high, bb)
                packed.append((bb, jnp.concatenate([kept - upper, upper], axis=1).astype(BF16)))
        copy_out(i).start()
        packed = jnp.concatenate([p for _, p in sorted(packed, key=lambda p: p[0])], axis=0)
        marks = target_ref[:, pl.ds(pl.multiple_of(i * block, block), block)]
        acc_ref[...] += dot(marks, packed)
        return carry

    steps = pre_ref.shape[0] // block
    lax.fori_loop(0, steps, step, 0)
    fresh = fresh_ref[...]
    inbound = jnp.concatenate([acc_ref[:, :LANES], acc_ref[:, LANES:]], axis=0).astype(BF16)
    hidden_n = dot(jnp.concatenate([fresh, inbound], axis=1), nw1_ref[...]) + nb1_ref[...]
    hidden_n = jnp.maximum(hidden_n, 0.0).astype(BF16)
    nb2 = nb2_ref[...]
    nb2 = nb2 - jnp.mean(nb2, axis=-1, keepdims=True)
    nw2 = nw2_ref[...].astype(F32)
    nw2 = twice((nw2 - jnp.mean(nw2, axis=-1, keepdims=True)).astype(BF16))
    centre = dot(side_by_side(hidden_n), nw2) + jnp.concatenate([nb2, nb2], axis=1)
    spreads = dot((centre * centre).astype(BF16), averages)
    normed = centre * lax.rsqrt(spreads + EPSILON)
    for k in range(2):
        rows = slice(k * nodes_half, (k + 1) * nodes_half)
        update = normed[:, k * LANES : (k + 1) * LANES] * ngain_ref[...] + nbias_ref[...]
        node_out_ref[rows, :] = (fresh[rows].astype(F32) + update).astype(BF16)
    for i in range(steps):
        copy_out(i).wait()


def outward(near_partner, far, d):
    rows = far.shape[0] // 2
    even_pair = (d // 2) % 2 == 0
    plus = jnp.concatenate([far[rows:], near_partner[rows:]], axis=0)
    minus = jnp.concatenate([far[:rows], near_partner[:rows]], axis=0)
    outer = swapped(
        jnp.where(even_pair, minus, plus), "dom", lambda i: i - 2 if i % 4 < 2 else i + 2
    )
    inner = swapped(
        jnp.where(even_pair, plus, minus), "dom", lambda i: i + 2 if i % 4 < 2 else i - 2
    )
    return outer, inner


def inward(near_partner, outer, inner, d):
    rows = near_partner.shape[0] // 2
    odd = d % 2 == 1
    even_pair = (d // 2) % 2 == 0
    before = jnp.where(even_pair, outer, inner)
    after = jnp.where(even_pair, inner, outer)
    return jnp.concatenate(
        [
            after[:rows],
            jnp.where(odd, after[rows:], near_partner[:rows]),
            jnp.where(odd, near_partner[rows:], before[rows:]),
            before[:rows],
        ],
        axis=0,
    )


def call(kernel, name, out_shape, limit, flops=10**9, **kw):
    return pl.pallas_call(
        kernel,
        out_shape=out_shape,
        name=name,
        compiler_params=pltpu.CompilerParams(vmem_limit_bytes=limit << 20),
        cost_estimate=pl.CostEstimate(flops=flops, bytes_accessed=10**6, transcendentals=0),
        **kw,
    )


VM = pl.BlockSpec(memory_space=pltpu.VMEM)
HBM = pl.BlockSpec(memory_space=pltpu.MemorySpace.HBM)


def like(*arrays):
    return [jax.ShapeDtypeStruct(a.shape, a.dtype) for a in arrays]


def body(
    node_latent, edge_latent, mig_send, mig_recv, halo_send, cross_send, senders, receivers, edge_live,
    edge_w1, edge_b1, edge_w2, edge_b2, edge_gain, edge_bias,
    node_w1, node_b1, node_w2, node_b2, node_gain, node_bias,
):
    n, latent = node_latent.shape
    edges = edge_latent.shape[0]
    d = lax.axis_index("dom")
    move = mig_send.shape[1]
    halo = halo_send.shape[1]
    cross = cross_send.shape[1]
    shape = jax.ShapeDtypeStruct
    row = lambda v: v.reshape(1, latent)
    tiles = lambda v: v.reshape(-1, LANES)

    near, far = call(
        leave_kernel,
        "leave",
        [shape((move // 2, latent), BF16)] * 2,
        4,
        in_specs=[HBM] * 2,
        scratch_shapes=[
            pltpu.VMEM(node_latent.shape, BF16),
            pltpu.VMEM(mig_send.shape, jnp.int32),
            pltpu.SemaphoreType.DMA((2,)),
        ],
    )(node_latent, mig_send)
    partner = swapped(near, "dom", lambda i: i ^ 1)
    args = (
        edge_latent, edge_w1, row(edge_b1), tiles(senders), tiles(receivers), tiles(edge_live),
        tiles(mig_recv), halo_send, cross_send,
    )
    own, w1, send, recv, live, mig, halo_index, cross_index = call(
        own_kernel,
        "own",
        [shape((edges, latent), F32)] + like(args[1], *args[3:]),
        10,
        in_specs=[VM] * 9 + [ANY],
    )(*args, near)
    partner, own, recv = lax.optimization_barrier((partner, own, recv))
    outer, inner = outward(partner, far, d)
    targets, table = call(
        target_kernel,
        "targets",
        [shape((n // 2, edges), BF16), shape((n // 2, 2 * latent), BF16)],
        10,
        in_specs=[VM, VM, ANY],
    )(recv, node_latent, partner)
    outer, inner, targets, table = lax.optimization_barrier((outer, inner, targets, table))
    arrived = inward(partner, outer, inner, d)

    fresh, near, far, cross_out = call(
        fresh_kernel,
        "fresh",
        [shape((n, latent), BF16)] + [shape((halo // 2, latent), BF16)] * 2 + [shape((cross, latent), BF16)],
        8,
    )(table, arrived, mig, halo_index, cross_index)
    partner = swapped(near, "dom", lambda i: i ^ 1)
    cross_in = lax.ppermute(cross_out, "grp", [(i, i ^ 1) for i in range(lax.axis_size("grp"))])
    (pre,) = call(
        functools.partial(pre_kernel, part=2), "received", [shape((edges, latent), F32)], 10,
        in_specs=[VM] * 4 + [ANY],
    )(own, fresh, recv, w1, near)
    partner, pre = lax.optimization_barrier((partner, pre))
    outer, inner = outward(partner, far, d)
    (pre,) = call(
        functools.partial(pre_kernel, part=1), "sent", [shape((edges, latent), F32)], 10,
        in_specs=[VM] * 4 + [ANY],
    )(pre, fresh, send, w1, partner)
    outer, inner, cross_in, pre = lax.optimization_barrier((outer, inner, cross_in, pre))
    halo_in = inward(partner, outer, inner, d)
    node_out, edge_out = call(
        edge_kernel,
        "edges",
        [shape((n, latent), BF16), shape((edges, latent), BF16)],
        16,
        flops=10**10,
        out_specs=[VM, ANY],
        scratch_shapes=[
            pltpu.VMEM((edges, latent), BF16),
            pltpu.VMEM((n // 2, 2 * latent), F32),
            pltpu.SemaphoreType.DMA((edges // EDGE_BLOCK,)),
        ],
    )(
        pre, edge_latent, fresh, halo_in, cross_in, send, recv, live, targets,
        w1, edge_w2, row(edge_b2), row(edge_gain), row(edge_bias),
        node_w1, row(node_b1), node_w2, row(node_b2), row(node_gain), row(node_bias),
    )
    return node_out, edge_out


def solution(mesh):
    split, split1, copied = P(("grp", "dom"), None), P(("grp", "dom")), P()
    placed = (
        split, split, split, split1, split, split, split1, split1, split1,
    ) + (copied,) * 12
    return jax.shard_map(
        body, mesh=mesh, in_specs=placed, out_specs=(split, split), check_vma=False
    )
```

time: 97.9 us -> 39.3 us (0.40)
  the two profiles are of different devices: /device:TPU:0 before, /device:TPU:12 now
where the time goes in v1:
time: 39.3 us; the launch traced here: 39.1 us
  Pallas kernels  20.9 us (53%)
  starting transfers between devices  13.2 us (34%)
  local copies, waits for them, and re-layouts  2.81 us (7%)
  between operations  1.16 us (3%)
  waiting for transfers between devices  0.93 us (2%)
    ppermute x6, starting transfers between devices, swapped(): return lax.ppermute(value, axis, pairs)  13.1 us
    pallas_call x1, Pallas kernels, body(): call(edge_kernel, 'edges', [shape((n, latent), BF16), shape((edges, laten...  9.15 us
    pallas_call x1, Pallas kernels, body(): call(functools.partial(pre_kernel, part=1), 'sent', [shape((edges, latent...  3.68 us
    pallas_call x1, Pallas kernels, body(): call(functools.partial(pre_kernel, part=2), 'received', [shape((edges, la...  3.66 us
    unnamed x46, local copies, waits for them, and re-layouts  2.79 us
    pallas_call x1, Pallas kernels, body(): call(target_kernel, 'targets', [shape((n // 2, edges), BF16), shape((n //...  1.6 us
    pallas_call x1, Pallas kernels, body(): call(own_kernel, 'own', [shape((edges, latent), F32)] + like(args[1], *ar...  1.38 us
    pallas_call x1, Pallas kernels, body(): call(fresh_kernel, 'fresh', [shape((n, latent), BF16)] + [shape((halo //...  1.06 us
  transfers between devices with their start and end apart: 7, of which 1 were waited for; matrix products, arithmetic and copies ran while one was open for 0% of the time, Pallas kernels for 26%

profile of v1, /device:TPU:12, one launch (start us, length us, event | category | flops | bytes accessed | tf_op | source)
XLA Modules:
  0.0 39.1 jit_solution(16924685712122644504)
XLA Ops:
  0.6 0.0 copy-start
  0.6 0.0 copy-start.2
  0.7 1.1 %copy-done.2 = bf16[1024,128]{1,0:T(8,128)(2,1)S(1)} copy-done((bf16[1024,128]{1,0:T(8,128)(2,1)S(1)}, bf16[1024,128]{1,0:T(8,128)(2,1)}, u32[]{:S(2)}) %copy-start.2) | copy-done | bytes 262168
  1.7 0.7 %copy-done.12 = s32[1,256]{1,0:T(1,128)S(1)} copy-done((s32[1,256]{1,0:T(1,128)S(1)}, s32[1,256]{1,0:T(1,128)}, u32[]{:S(2)}) %copy-start.12) | copy-done | bytes 1048
  2.4 0.4 %leave.1 = (bf16[128,128]{1,0:T(8,128)(2,1)S(1)}, bf16[128,128]{1,0:T(8,128)(2,1)S(1)}) custom-call(bf16[1024,128]{1,0:T(8,128)(2,1)S(1)} %copy-done.2, s32[1,256]{1,0:T(1,128)S(1)} %copy-done.12), custom_call_target="tpu_custom_call" | custom-call | flops 1000000000 | bytes 1000000 | tf_op jit(solution)/shard_map/leave/pallas_call | solution.py:325
  2.8 1.6 %collective-permute-start = (bf16[128,128]{1,0:T(8,128)(2,1)S(1)}, bf16[128,128]{1,0:T(8,128)(2,1)S(1)}, u32[]{:S(2)}, u32[]{:S(2)}) collective-permute-start(bf16[128,128]{1,0:T(8,128)(2,1)S(1)} %get-tuple-element.32._), channel_id=1, source_target_pairs={{0,1},{1,0},{2,3},{3,2},{4,5},{5,4},{6,7},{7,6},{8,9},{9,8},{10,11... | collective-permute-start | bytes 98312 | tf_op jit(solution)/shard_map/ppermute | solution.py:29
  4.5 1.4 %own.1 = (f32[6144,128]{1,0:T(8,128)S(1)}, bf16[384,128]{1,0:T(8,128)(2,1)S(1)}, s32[48,128]{1,0:T(8,128)S(1)}, s32[48,128]{1,0:T(8,128)S(1)}, s32[48,128]{1,0:T...) custom-call(bf16[6144,128]{1,0:T(8,128)(2,1)S(1)} %copy-done, ...), custom_call_target="tpu_custom_call" | custom-call | flops 1000000000 | bytes 1000000 | tf_op jit(solution)/shard_map/own/pallas_call | solution.py:342
  5.9 0.9 %collective-permute-done._ = bf16[128,128]{1,0:T(8,128)(2,1)S(1)} collective-permute-done((bf16[128,128]{1,0:T(8,128)(2,1)S(1)}, bf16[128,128]{1,0:T(8,128)(2,1)S(1)}, u32[]{:S(2)}, u32[]{:S(2)}) %collective-permute-start) | collective-permute-done | bytes 32800 | tf_op jit(solution)/shard_map/ppermute | solution.py:29
  6.9 0.6 %collective-permute-start.2 = (bf16[128,128]{1,0:T(8,128)(2,1)S(1)}, bf16[128,128]{1,0:T(8,128)(2,1)S(1)}, u32[]{:S(2)}, u32[]{:S(2)}) collective-permute-start(bf16[128,128]{1,0:T(8,128)(2,1)S(1)} %get-tuple-element.62), channel_id=1, source_target_pairs={{0,2},{1,3},{2,0},{3,1},{4,6},{5,7},{6,4},{7,5},{8,10},{9,11},{10,... | collective-permute-start | bytes 98312 | tf_op jit(solution)/shard_map/ppermute | solution.py:29
  7.4 4.4 %collective-permute-start.1 = (bf16[128,128]{1,0:T(8,128)(2,1)S(1)}, bf16[128,128]{1,0:T(8,128)(2,1)S(1)}, u32[]{:S(2)}, u32[]{:S(2)}) collective-permute-start(bf16[128,128]{1,0:T(8,128)(2,1)S(1)} %get-tuple-element.63), channel_id=1, source_target_pairs={{0,0},{1,1},{2,4},{3,5},{4,2},{5,3},{6,8},{7,9},{8,6},{9,7},{10,12... | collective-permute-start | bytes 98312 | tf_op jit(solution)/shard_map/ppermute | solution.py:29
  11.9 0.9 %copy-done.3 = bf16[1024,128]{1,0:T(8,128)(2,1)S(1)} copy-done((bf16[1024,128]{1,0:T(8,128)(2,1)S(1)}, bf16[1024,128]{1,0:T(8,128)(2,1)}, u32[]{:S(2)}) %copy-start.3) | copy-done | bytes 262168
  12.8 1.6 %targets.1 = (bf16[512,6144]{1,0:T(8,128)(2,1)S(1)}, bf16[512,256]{1,0:T(8,128)(2,1)S(1)}) custom-call(s32[48,128]{1,0:T(8,128)S(1)} %get-tuple-element.36.recv_ref.index_ref, bf16[1024,128]{1,0:T(8,128)(2,1)S(1)} %copy-done.3, bf16[128,128]{1,0:T(8,128)(2,1)S(1)} %collective-permute-done._), custom_call_target="tpu_custom_call" | custom-call | flops 1000000000 | bytes 1000000 | tf_op jit(solution)/shard_map/targets/pallas_call | solution.py:351
  14.5 1.1 %fresh.1 = (bf16[1024,128]{1,0:T(8,128)(2,1)S(1)}, bf16[64,128]{1,0:T(8,128)(2,1)S(1)}, bf16[64,128]{1,0:T(8,128)(2,1)S(1)}, bf16[32,128]{1,0:T(8,128)(2,1)S(1)}) custom-call(bf16[512,256]{1,0:T(8,128)(2,1)S(1)} %get-tuple-element.39.table_ref, bf16[256,128]{1,0:T(8,128)(2,1)S(1)} %pad_maximum_fusion.arrived_ref, s32[8,128]{1,0:T(8,128)S(1)} %get-tuple-element.42.recv_ref, ...), custom_call_target="tpu_custom_call" | custom-call | flops 1000000000 | bytes 1000000 | tf_op jit(solution)/shard_map/fresh/pallas_call | solution.py:361
  15.6 0.1 collective-permute-start.6
  15.7 1.6 %collective-permute-start.3 = (bf16[64,128]{1,0:T(8,128)(2,1)S(1)}, bf16[64,128]{1,0:T(8,128)(2,1)S(1)}, u32[]{:S(2)}, u32[]{:S(2)}) collective-permute-start(bf16[64,128]{1,0:T(8,128)(2,1)S(1)} %get-tuple-element.46._), channel_id=1, source_target_pairs={{0,1},{1,0},{2,3},{3,2},{4,5},{5,4},{6,7},{7,6},{8,9},{9,8},{10,11... | collective-permute-start | bytes 49160 | tf_op jit(solution)/shard_map/ppermute | solution.py:29
  17.2 3.7 %received.1.before_ref = f32[6144,128]{1,0:T(8,128)S(1)} custom-call(f32[6144,128]{1,0:T(8,128)S(1)} %get-tuple-element.47.before_ref, bf16[1024,128]{1,0:T(8,128)(2,1)S(1)} %get-tuple-element.48.fresh_ref, s32[48,128]{1,0:T(8,128)S(1)} %get-tuple-element.36.recv_ref.index_ref, bf16[384,128]{1,0:T(8,128)(2,1)S(1)} %get-tuple-element.49.w_ref.w1_ref, ...), custom_call_target="tpu_custom_call" | custom-call | flops 1000000000 | bytes 1000000 | tf_op jit(solution)/shard_map/received/pallas_call | solution.py:369
  20.9 1.3 %collective-permute-start.5 = (bf16[64,128]{1,0:T(8,128)(2,1)S(1)}, bf16[64,128]{1,0:T(8,128)(2,1)S(1)}, u32[]{:S(2)}, u32[]{:S(2)}) collective-permute-start(bf16[64,128]{1,0:T(8,128)(2,1)S(1)} %get-tuple-element.66), channel_id=1, source_target_pairs={{0,2},{1,3},{2,0},{3,1},{4,6},{5,7},{6,4},{7,5},{8,10},{9,11},{10,... | collective-permute-start | bytes 49160 | tf_op jit(solution)/shard_map/ppermute | solution.py:29
  22.2 3.7 %collective-permute-start.4 = (bf16[64,128]{1,0:T(8,128)(2,1)S(1)}, bf16[64,128]{1,0:T(8,128)(2,1)S(1)}, u32[]{:S(2)}, u32[]{:S(2)}) collective-permute-start(bf16[64,128]{1,0:T(8,128)(2,1)S(1)} %get-tuple-element.67), channel_id=1, source_target_pairs={{0,0},{1,1},{2,4},{3,5},{4,2},{5,3},{6,8},{7,9},{8,6},{9,7},{10,12... | collective-permute-start | bytes 49160 | tf_op jit(solution)/shard_map/ppermute | solution.py:29
  25.9 0.0 copy-start.5
  26.0 0.0 copy-start.6
  26.0 0.0 copy-start.17
  26.0 0.0 copy-start.18
  26.1 3.7 %sent.1.pre_ref = f32[6144,128]{1,0:T(8,128)S(1)} custom-call(f32[6144,128]{1,0:T(8,128)S(1)} %received.1.before_ref, bf16[1024,128]{1,0:T(8,128)(2,1)S(1)} %get-tuple-element.48.fresh_ref, s32[48,128]{1,0:T(8,128)S(1)} %get-tuple-element.53.index_ref.send_ref, bf16[384,128]{1,0:T(8,128)(2,1)S(1)} %get-tuple-element.49.w_ref.w1_ref, ...), custom_call_target="tpu_custom_call" | custom-call | flops 1000000000 | bytes 1000000 | tf_op jit(solution)/shard_map/sent/pallas_call | solution.py:375
  29.9 9.1 %edges.1 = (bf16[1024,128]{1,0:T(8,128)(2,1)}, bf16[6144,128]{1,0:T(8,128)(2,1)}) custom-call(f32[6144,128]{1,0:T(8,128)S(1)} %sent.1.pre_ref, bf16[6144,128]{1,0:T(8,128)(2,1)S(1)} %copy-done.1, bf16[1024,128]{1,0:T(8,128)(2,1)S(1)} %get-tuple-element.48.fresh_ref, bf16[128,128]{1,0:T(8,128)(2,1)S(1)} %pad_maximum_fusion.3.halo_ref, ...), custom_call_target="tpu_custom_call" | custom-call | flops 10000000000 | bytes 1000000 | tf_op jit(solution)/shard_map/edges/pallas_call | solution.py:381
  (55 shorter events, 0.2 us)
Async XLA Ops:
  0.6 3.8 %copy-start = (bf16[6144,128]{1,0:T(8,128)(2,1)S(1)}, bf16[6144,128]{1,0:T(8,128)(2,1)}, u32[]{:S(2)}) copy-start(bf16[6144,128]{1,0:T(8,128)(2,1)} %edge_ref.3) | copy-start | bytes 4718596
  2.4 2.0 %copy-start.10 = (s32[6144]{0:T(1024)S(1)}, s32[6144]{0:T(1024)}, u32[]{:S(2)}) copy-start(s32[6144]{0:T(1024)} %param.29) | copy-start | bytes 73732
  2.4 2.0 %copy-start.11 = (s32[1024]{0:T(1024)S(1)}, s32[1024]{0:T(1024)}, u32[]{:S(2)}) copy-start(s32[1024]{0:T(1024)} %param.24) | copy-start | bytes 12292
  2.4 2.0 %copy-start.13 = (f32[128]{0:T(128)S(1)}, f32[128]{0:T(128)}, u32[]{:S(2)}) copy-start(f32[128]{0:T(128)} %param.31) | copy-start | bytes 1540
  2.4 2.0 %copy-start.14 = (s32[1,128]{1,0:T(1,128)S(1)}, s32[1,128]{1,0:T(1,128)}, u32[]{:S(2)}) copy-start(s32[1,128]{1,0:T(1,128)} %halo_ref.1) | copy-start | bytes 1540
  2.4 2.0 %copy-start.15 = (s32[1,32]{1,0:T(1,128)S(1)}, s32[1,32]{1,0:T(1,128)}, u32[]{:S(2)}) copy-start(s32[1,32]{1,0:T(1,128)} %cross_ref.1) | copy-start | bytes 388
  2.8 4.0 %collective-permute-start = (bf16[128,128]{1,0:T(8,128)(2,1)S(1)}, bf16[128,128]{1,0:T(8,128)(2,1)S(1)}, u32[]{:S(2)}, u32[]{:S(2)}) collective-permute-start(bf16[128,128]{1,0:T(8,128)(2,1)S(1)} %get-tuple-element.32._), channel_id=1, source_target_pairs={{0,1},{1,0},{2,3},{3,2},{4,5},{5,4},{6,7},{7,6},{8,9},{9,8},{10,11... | collective-permute-start | bytes 98312 | tf_op jit(solution)/shard_map/ppermute | solution.py:29
  6.9 7.6 %collective-permute-start.2 = (bf16[128,128]{1,0:T(8,128)(2,1)S(1)}, bf16[128,128]{1,0:T(8,128)(2,1)S(1)}, u32[]{:S(2)}, u32[]{:S(2)}) collective-permute-start(bf16[128,128]{1,0:T(8,128)(2,1)S(1)} %get-tuple-element.62), channel_id=1, source_target_pairs={{0,2},{1,3},{2,0},{3,1},{4,6},{5,7},{6,4},{7,5},{8,10},{9,11},{10,... | collective-permute-start | bytes 98312 | tf_op jit(solution)/shard_map/ppermute | solution.py:29
  7.4 7.0 %collective-permute-start.1 = (bf16[128,128]{1,0:T(8,128)(2,1)S(1)}, bf16[128,128]{1,0:T(8,128)(2,1)S(1)}, u32[]{:S(2)}, u32[]{:S(2)}) collective-permute-start(bf16[128,128]{1,0:T(8,128)(2,1)S(1)} %get-tuple-element.63), channel_id=1, source_target_pairs={{0,0},{1,1},{2,4},{3,5},{4,2},{5,3},{6,8},{7,9},{8,6},{9,7},{10,12... | collective-permute-start | bytes 98312 | tf_op jit(solution)/shard_map/ppermute | solution.py:29
  15.6 14.2 %collective-permute-start.6 = (bf16[32,128]{1,0:T(8,128)(2,1)S(1)}, bf16[32,128]{1,0:T(8,128)(2,1)S(1)}, u32[]{:S(2)}, u32[]{:S(2)}) collective-permute-start(bf16[32,128]{1,0:T(8,128)(2,1)S(1)} %get-tuple-element.51), channel_id=1, source_target_pairs={{0,16},{16,0},{1,17},{17,1},{2,18},{18,2},{3,19},{19,3},{4,20},{20... | collective-permute-start | bytes 24584 | tf_op jit(solution)/shard_map/ppermute | solution.py:368
  15.7 5.2 %collective-permute-start.3 = (bf16[64,128]{1,0:T(8,128)(2,1)S(1)}, bf16[64,128]{1,0:T(8,128)(2,1)S(1)}, u32[]{:S(2)}, u32[]{:S(2)}) collective-permute-start(bf16[64,128]{1,0:T(8,128)(2,1)S(1)} %get-tuple-element.46._), channel_id=1, source_target_pairs={{0,1},{1,0},{2,3},{3,2},{4,5},{5,4},{6,7},{7,6},{8,9},{9,8},{10,11... | collective-permute-start | bytes 49160 | tf_op jit(solution)/shard_map/ppermute | solution.py:29
  20.9 8.8 %collective-permute-start.5 = (bf16[64,128]{1,0:T(8,128)(2,1)S(1)}, bf16[64,128]{1,0:T(8,128)(2,1)S(1)}, u32[]{:S(2)}, u32[]{:S(2)}) collective-permute-start(bf16[64,128]{1,0:T(8,128)(2,1)S(1)} %get-tuple-element.66), channel_id=1, source_target_pairs={{0,2},{1,3},{2,0},{3,1},{4,6},{5,7},{6,4},{7,5},{8,10},{9,11},{10,... | collective-permute-start | bytes 49160 | tf_op jit(solution)/shard_map/ppermute | solution.py:29
  22.2 7.6 %collective-permute-start.4 = (bf16[64,128]{1,0:T(8,128)(2,1)S(1)}, bf16[64,128]{1,0:T(8,128)(2,1)S(1)}, u32[]{:S(2)}, u32[]{:S(2)}) collective-permute-start(bf16[64,128]{1,0:T(8,128)(2,1)S(1)} %get-tuple-element.67), channel_id=1, source_target_pairs={{0,0},{1,1},{2,4},{3,5},{4,2},{5,3},{6,8},{7,9},{8,6},{9,7},{10,12... | collective-permute-start | bytes 49160 | tf_op jit(solution)/shard_map/ppermute | solution.py:29
  25.9 3.9 %copy-start.1 = (bf16[6144,128]{1,0:T(8,128)(2,1)S(1)}, bf16[6144,128]{1,0:T(8,128)(2,1)}, u32[]{:S(2)}) copy-start(bf16[6144,128]{1,0:T(8,128)(2,1)} %edge_ref.3) | copy-start | bytes 4718596
  25.9 3.9 %copy-start.5 = (bf16[256,128]{1,0:T(8,128)(2,1)S(1)}, bf16[256,128]{1,0:T(8,128)(2,1)}, u32[]{:S(2)}) copy-start(bf16[256,128]{1,0:T(8,128)(2,1)} %nw1_ref.1) | copy-start | bytes 196612
  26.0 3.9 %copy-start.6 = (bf16[128,128]{1,0:T(8,128)(2,1)S(1)}, bf16[128,128]{1,0:T(8,128)(2,1)}, u32[]{:S(2)}) copy-start(bf16[128,128]{1,0:T(8,128)(2,1)} %w2_ref.1) | copy-start | bytes 98308
  26.0 3.9 %copy-start.7 = (bf16[128,128]{1,0:T(8,128)(2,1)S(1)}, bf16[128,128]{1,0:T(8,128)(2,1)}, u32[]{:S(2)}) copy-start(bf16[128,128]{1,0:T(8,128)(2,1)} %nw2_ref.1) | copy-start | bytes 98308
  26.0 3.9 %copy-start.16 = (f32[128]{0:T(128)S(1)}, f32[128]{0:T(128)}, u32[]{:S(2)}) copy-start(f32[128]{0:T(128)} %param.33) | copy-start | bytes 1540
  26.0 3.9 %copy-start.17 = (f32[128]{0:T(128)S(1)}, f32[128]{0:T(128)}, u32[]{:S(2)}) copy-start(f32[128]{0:T(128)} %param.34) | copy-start | bytes 1540
  26.0 3.9 %copy-start.18 = (f32[128]{0:T(128)S(1)}, f32[128]{0:T(128)}, u32[]{:S(2)}) copy-start(f32[128]{0:T(128)} %param.35) | copy-start | bytes 1540
  26.0 3.9 %copy-start.19 = (f32[128]{0:T(128)S(1)}, f32[128]{0:T(128)}, u32[]{:S(2)}) copy-start(f32[128]{0:T(128)} %param.37) | copy-start | bytes 1540
  26.0 3.9 %copy-start.20 = (f32[128]{0:T(128)S(1)}, f32[128]{0:T(128)}, u32[]{:S(2)}) copy-start(f32[128]{0:T(128)} %param.39) | copy-start | bytes 1540
  26.0 3.9 %copy-start.21 = (f32[128]{0:T(128)S(1)}, f32[128]{0:T(128)}, u32[]{:S(2)}) copy-start(f32[128]{0:T(128)} %param.40) | copy-start | bytes 1540
  26.1 3.9 %copy-start.22 = (f32[128]{0:T(128)S(1)}, f32[128]{0:T(128)}, u32[]{:S(2)}) copy-start(f32[128]{0:T(128)} %param.41) | copy-start | bytes 1540
  (6 other events, 8.8 us)
